TPU v7x, 32 devices: a whole 2x2x4 slice. The times are simulated.
32 devices in a mesh: seq: 8 (over z, x), head: 4 (over y, core).
Axes of the slice: x: 2, y: 2, z: 4, core: 2. Of those that a mesh axis runs over, the one named last changes fastest.
Arguments:
- tokens: bfloat16 [2048, 3584], P('seq'), may hold values from -16 to 16
- length: int32 [1], replicated, may hold values from 512 to 2048
- in_gain: float32 [3584], replicated, may hold values from 0.5 to 1.5
- q_weight: bfloat16 [3584, 3584], P(None, 'head'), may hold values from -0.09375 to 0.09375
- q_bias: float32 [3584], P('head'), may hold values from -60 to 60
- k_weight: bfloat16 [3584, 512], P(None, 'head'), may hold values from -0.09375 to 0.09375
- k_bias: float32 [512], P('head'), may hold values from -60 to 60
- v_weight: bfloat16 [3584, 512], P(None, 'head'), may hold values from -0.09375 to 0.09375
- v_bias: float32 [512], P('head'), may hold values from -2 to 2
- o_weight: bfloat16 [3584, 3584], P('head'), may hold values from -0.125 to 0.125
- final_gain: float32 [3584], P('head'), may hold values from 0.5 to 1.5
Outputs:
- hidden: bfloat16 [2048, 3584], P('seq', 'head')
- embedding: float32 [3584], P('head')
All inputs are finite; a program needn't handle non-finite values.
Results may differ from a plain program's by a relative error of at most 0.0075.
The roundings to bfloat16 on the way count: a program that leaves them out, or rounds other values in their place, can miss the bound.
Values may be sent and summed in bfloat16 or wider, within the bound.
A program may use at most 192 MiB of HBM per device.

v0:
```python
import jax
import jax.numpy as jnp
from jax import lax
from jax.sharding import PartitionSpec as P

D = 3584
HEAD_DIM = 128
rope_base = 1000000.0
epsilon = 1e-06


def rms_norm(inputs, gain):
    inputs = inputs.astype(jnp.float32)
    return inputs * lax.rsqrt(jnp.mean(inputs * inputs, axis=-1, keepdims=True) + epsilon) * gain


def rope_tables(positions):
    half_dim = HEAD_DIM // 2
    inverse = rope_base ** (-(jnp.arange(half_dim, dtype=jnp.float32) * 2.0) / HEAD_DIM)
    angles = positions.astype(jnp.float32)[:, None] * inverse[None, :]
    angles = jnp.concatenate([angles, angles], axis=1)
    return (jnp.cos(angles), jnp.sin(angles))


def rotate(inputs, cosine, sine):
    half_dim = HEAD_DIM // 2
    turned = jnp.concatenate([-inputs[..., half_dim:], inputs[..., :half_dim]], axis=-1)
    return inputs * cosine[:, None, :] + turned * sine[:, None, :]


def key_scores(queries, key_block):
    return lax.dot_general(
        queries, key_block, (((1,), (1,)), ((), ())), preferred_element_type=jnp.float32
    )


def body(
    tokens,
    length,
    in_gain,
    q_weight,
    q_bias,
    k_weight,
    k_bias,
    v_weight,
    v_bias,
    o_weight,
    final_gain,
):
    tok_rows = tokens.shape[0]
    head_count = q_weight.shape[1] // HEAD_DIM
    offset = lax.axis_index("seq") * tok_rows
    limit = length[0]
    positions = offset + jnp.arange(tok_rows, dtype=jnp.int32)
    normed = rms_norm(tokens, in_gain).astype(jnp.bfloat16)
    cosine, sine = rope_tables(positions)
    query = jnp.dot(normed, q_weight, preferred_element_type=jnp.float32) + q_bias
    query = rotate(query.reshape(tok_rows, head_count, HEAD_DIM), cosine, sine) * HEAD_DIM ** (-0.5)
    query = query.astype(jnp.bfloat16).reshape(tok_rows * head_count, HEAD_DIM)
    keys = jnp.dot(normed, k_weight, preferred_element_type=jnp.float32) + k_bias
    keys = (
        rotate(keys.reshape(tok_rows, 1, HEAD_DIM), cosine, sine)
        .astype(jnp.bfloat16)
        .reshape(tok_rows, HEAD_DIM)
    )
    values = (jnp.dot(normed, v_weight, preferred_element_type=jnp.float32) + v_bias).astype(
        jnp.bfloat16
    )
    q_rows = query.shape[0]

    def absorb(carry, piece):
        top, total, accum = carry
        k_piece, v_piece = piece
        count = k_piece.shape[0]
        live = jnp.arange(count, dtype=jnp.int32) < limit
        scores = jnp.where(live[None, :], key_scores(query, k_piece), -1e30)
        new_top = jnp.maximum(top, jnp.max(scores, axis=1))
        weights = jnp.where(live[None, :], jnp.exp(scores - new_top[:, None]), 0.0)
        total = jnp.sum(weights, axis=1)
        accum = jnp.dot(weights.astype(jnp.bfloat16), v_piece, preferred_element_type=jnp.float32)
        return (new_top, total, accum)

    initial = (
        jnp.full((q_rows,), -1e30, jnp.float32),
        jnp.zeros((q_rows,), jnp.float32),
        jnp.zeros((q_rows, HEAD_DIM), jnp.float32),
    )
    piece = (
        lax.all_gather(keys, "seq", axis=0, tiled=True),
        lax.all_gather(values, "seq", axis=0, tiled=True),
    )

    def update(state):
        return absorb(state, piece)

    def unchanged(state):
        return state

    top, total, accum = lax.cond(jnp.int32(0) < limit, update, unchanged, initial)
    attended = (
        (accum / total[:, None]).astype(jnp.bfloat16).reshape(tok_rows, head_count * HEAD_DIM)
    )
    mixed = jnp.dot(attended, o_weight, preferred_element_type=jnp.float32)
    width_share = D // lax.axis_size("head")
    column = lax.axis_index("head") * width_share
    shared = lax.psum_scatter(
        mixed.astype(jnp.bfloat16), "head", scatter_dimension=1, tiled=True
    ).astype(jnp.float32)
    hidden_full = (
        lax.dynamic_slice_in_dim(tokens, column, width_share, 1).astype(jnp.float32) + shared
    )
    squares = lax.psum(jnp.sum(hidden_full * hidden_full, axis=1), "head")
    final = hidden_full * lax.rsqrt(squares[:, None] / D + epsilon) * final_gain
    row_live = positions < limit
    local_sum = jnp.sum(jnp.where(row_live[:, None], final, 0.0), axis=0)
    pooled_sum = lax.psum(local_sum, "seq")
    mean = pooled_sum / limit.astype(jnp.float32)
    power = lax.psum(jnp.sum(mean * mean), "head")
    embedding = mean * lax.rsqrt(power / D + epsilon)
    return (hidden_full.astype(jnp.bfloat16), embedding)


def solution(mesh):
    in_specs = (
        P("seq", None),
        P(),
        P(),
        P(None, "head"),
        P("head"),
        P(None, "head"),
        P("head"),
        P(None, "head"),
        P("head"),
        P("head", None),
        P("head"),
    )
    out_specs = (P("seq", "head"), P("head"))
    return jax.shard_map(body, mesh=mesh, in_specs=in_specs, out_specs=out_specs, check_vma=False)
```

profile of v0, /device:TPU:0, one launch (start us, length us, event | category | flops | bytes accessed | tf_op | source)
XLA Modules:
  0.0 211.3 jit_solution(12068621012374544557)
XLA Ops:
  7.2 2.0 fusion.7
  9.3 6.5 %convolution_add_fusion = f32[256,896]{1,0:T(8,128)} fusion(bf16[3584,896]{1,0:T(8,128)(2,1)} %param.16, f32[896]{0:T(1024)} %param.17, bf16[256,3584]{1,0:T(8,128)(2,1)} %param.13, f32[3584]{0:T(1024)} %param.15, f32[256]{0:T(256)S(1)} %add_rsqrt_fusion.1), kind=kOutput, calls=%fused_computation.16 | convolution fusion | flops 1648066560 | bytes 9193984 | tf_op jit(solution)/shard_map/dot_general | solution.py:57
  15.7 2.6 %copy.23 = f32[256,896]{0,1:T(8,128)} copy(f32[256,896]{1,0:T(8,128)} %convolution_add_fusion) | data formatting | bytes 1835008 | tf_op jit(solution)/shard_map/add | solution.py:57
  18.3 2.2 %reshape.119 = f32[1792,128]{1,0:T(8,128)} reshape(f32[256,896]{1,0:T(8,128)} %convolution_add_fusion) | data formatting | bytes 1835008 | tf_op jit(solution)/shard_map/reshape | solution.py:58
  22.2 1.1 fusion.18
  23.5 33.5 %all_gather.6 = bf16[2048,128]{0,1:T(8,128)(2,1)S(1)} all-gather(bf16[256,128]{0,1:T(8,128)(2,1)} %get-tuple-element.38), channel_id=1, replica_groups=mesh['seq'=8,'head'=4] {'seq'}, dimensions={0}, use_global_device_ids=true | all-gather | bytes 589824 | tf_op jit(solution)/shard_map/all_gather | solution.py:89
  57.0 1.9 fusion.10
  58.9 33.4 %all_gather.7 = bf16[2048,128]{1,0:T(8,128)(2,1)} all-gather(bf16[256,128]{1,0:T(8,128)(2,1)S(1)} %fusion.10), channel_id=1, replica_groups=mesh['seq'=8,'head'=4] {'seq'}, dimensions={0}, use_global_device_ids=true | all-gather | bytes 589824 | tf_op jit(solution)/shard_map/all_gather | solution.py:90
  93.6 1.0 concatenate.28
  95.8 1.1 mul.134
  96.8 1.4 copy.25
  98.3 1.0 concatenate.29
  99.3 2.4 %fusion.13 = bf16[1792,128]{1,0:T(8,128)(2,1)S(1)} fusion(f32[1792,128]{1,0:T(8,128)} %mul.134, f32[1792,64]{1,0:T(8,128)} %concatenate.29, f32[1792,64]{1,0:T(8,128)} %concatenate.28, f32[1792,128]{1,0:T(8,128)S(1)} %copy-done.3, f32[1792,128]{1,0:T(8,128)} %mul.131), kind=kLoop, calls=%fused_computation.23 | loop fusion | flops 1376256 | bytes 4128768 | tf_op jit(solution)/shard_map/convert_element_type | solution.py:59
  101.7 22.9 %conditional.1 = (f32[1792]{0:T(1024)S(1)}, f32[1792,128]{1,0:T(8,128)S(1)}) conditional(s32[]{:T(128)} %convert_element_type.49, () %tuple.16, (s32[]{:T(128)}, bf16[1792,128]{1,0:T(8,128)(2,1)S(1)}, bf16[2048,128]{0,1:T(8,128)(2,1)S(1)}, bf16[2048,128]{1,0:T(8,128)(2,1)S(1)}) %tuple.32), branch_computations={%region_1.0_spmd, %region_2.5_spmd} | conditional | flops 1915748608 | bytes 46516244 | solution.py:99
  102.6 7.3 %select_reduce_fusion = (f32[1792]{0:T(1024)S(1)}, f32[1792,2048]{1,0:T(8,128)}) fusion(pred[2048]{0:T(1024)(128)(4,1)S(1)} %iota_compare_fusion, bf16[1792,128]{1,0:T(8,128)(2,1)S(1)} %get-tuple-element.9, bf16[2048,128]{0,1:T(8,128)(2,1)S(1)} %get-tuple-element.28), kind=kOutput, calls=%fused_computation.1 | convolution fusion | flops 946862336 | bytes 15672320 | tf_op jit(solution)/shard_map/cond/branch_1_fun/dot_general | solution.py:32
  109.9 8.2 %fusion.1 = f32[1792]{0:T(1024)S(1)} fusion(f32[1792,2048]{1,0:T(8,128)} %get-tuple-element.31, f32[1792]{0:T(1024)S(1)} %broadcast_maximum_fusion, pred[2048]{0:T(1024)(128)(4,1)S(1)} %iota_compare_fusion), kind=kLoop, calls=%fused_computation.3 | loop fusion | flops 14678272 | bytes 14696448 | tf_op jit(solution)/shard_map/cond/branch_1_fun/reduce_sum | solution.py:79
  118.0 6.6 %fusion.2 = f32[1792,128]{1,0:T(8,128)S(1)} fusion(bf16[2048,128]{1,0:T(8,128)(2,1)S(1)} %get-tuple-element.11, f32[1792,2048]{1,0:T(8,128)} %get-tuple-element.31, f32[1792]{0:T(1024)S(1)} %broadcast_maximum_fusion, pred[2048]{0:T(1024)(128)(4,1)S(1)} %iota_compare_fusion), kind=kOutput, calls=%fused_computation.4 | convolution fusion | flops 954204160 | bytes 16131072 | tf_op jit(solution)/shard_map/cond/branch_1_fun/dot_general | solution.py:80
  125.4 6.1 %convolution_convert_fusion = bf16[256,3584]{1,0:T(8,128)(2,1)} fusion(bf16[256,896]{1,0:T(8,128)(2,1)S(1)} %reshape.122, bf16[896,3584]{1,0:T(8,128)(2,1)} %param.22), kind=kOutput, calls=%fused_computation.10 | convolution fusion | flops 1645084672 | bytes 8716288 | tf_op jit(solution)/shard_map/dot_general | solution.py:103
  131.6 4.0 %copy.29 = bf16[256,3584]{0,1:T(8,128)(2,1)} copy(bf16[256,3584]{1,0:T(8,128)(2,1)} %convolution_convert_fusion) | data formatting | bytes 3670016
  135.6 30.9 %reduce-scatter.4.cloned.1.call-done = bf16[896,256]{1,0:T(8,128)(2,1)} async-done(((bf16[3584,256]{1,0:T(8,128)(2,1)}), bf16[896,256]{1,0:T(8,128)(2,1)}) %reduce-scatter.4.cloned.1.call-update) | async-done | bytes 458768
  166.5 1.3 copy.30
  168.0 5.8 %psum.21 = f32[256]{0:T(256)S(1)} all-reduce(f32[256]{0:T(256)S(1)} %multiply_reduce_fusion), channel_id=1, replica_groups=mesh['seq'=8,'head'=4] {'head'}, use_global_device_ids=true, to_apply=%region_7.8 | all-reduce | flops 256 | bytes 2048 | tf_op jit(solution)/shard_map/psum | solution.py:112
  174.8 21.5 %psum.22 = f32[896]{0:T(1024)S(1)} all-reduce(f32[896]{0:T(1024)S(1)} %get-tuple-element.32), channel_id=1, replica_groups=mesh['seq'=8,'head'=4] {'seq'}, use_global_device_ids=true, to_apply=%region_9.10 | all-reduce | flops 896 | bytes 7168 | tf_op jit(solution)/shard_map/psum | solution.py:116
  196.9 6.3 %psum.23 = f32[]{:T(128)} all-reduce(f32[]{:T(128)} %multiply_reduce_fusion.1), channel_id=1, replica_groups=mesh['seq'=8,'head'=4] {'head'}, use_global_device_ids=true, to_apply=%region_11.12 | all-reduce | flops 1 | bytes 8 | tf_op jit(solution)/shard_map/psum | solution.py:118
  (45 shorter events, 7.6 us)
Async XLA Ops:
  7.2 14.0 %copy-start = (bf16[3584,128]{1,0:T(8,128)(2,1)S(1)}, bf16[3584,128]{1,0:T(8,128)(2,1)}, u32[]{:S(2)}) copy-start(bf16[3584,128]{1,0:T(8,128)(2,1)} %param.18) | copy-start | bytes 2752516
  7.2 159.3 %reduce-scatter.4.cloned.1.call-start = ((), (), s32[]{:S(2)}) async-start(), calls=%async_computation.1 | async-start | bytes 2293760
  15.7 5.4 %copy-start.1 = (bf16[256,3584]{1,0:T(8,128)(2,1)S(1)}, bf16[256,3584]{1,0:T(8,128)(2,1)}, u32[]{:S(2)}) copy-start(bf16[256,3584]{1,0:T(8,128)(2,1)} %param.13) | copy-start | bytes 5505028
  15.7 5.5 %copy-start.7 = (f32[3584]{0:T(1024)S(1)}, f32[3584]{0:T(1024)}, u32[]{:S(2)}) copy-start(f32[3584]{0:T(1024)} %param.15) | copy-start | bytes 43012
  15.7 5.5 %copy-start.8 = (f32[128]{0:T(128)S(1)}, f32[128]{0:T(128)}, u32[]{:S(2)}) copy-start(f32[128]{0:T(128)} %param.19) | copy-start | bytes 1540
  18.3 38.7 %copy-start.9 = (f32[128]{0:T(128)S(1)}, f32[128]{0:T(128)}, u32[]{:S(2)}) copy-start(f32[128]{0:T(128)} %param.21) | copy-start | bytes 1540
  23.5 68.8 %copy-start.4 = (f32[256,896]{0,1:T(8,128)S(1)}, f32[256,896]{0,1:T(8,128)}, u32[]{:S(2)}) copy-start(f32[256,896]{0,1:T(8,128)} %copy.23) | copy-start | bytes 2752516
  95.7 3.6 %copy-start.3 = (f32[1792,128]{1,0:T(8,128)S(1)}, f32[1792,128]{1,0:T(8,128)}, u32[]{:S(2)}) copy-start(f32[1792,128]{1,0:T(8,128)} %reshape.119) | copy-start | bytes 2752516
  99.3 2.4 %copy-start.5 = (bf16[2048,128]{1,0:T(8,128)(2,1)S(1)}, bf16[2048,128]{1,0:T(8,128)(2,1)}, u32[]{:S(2)}) copy-start(bf16[2048,128]{1,0:T(8,128)(2,1)} %all_gather.7) | copy-start | bytes 1572868
  131.6 36.2 %copy-start.2 = (bf16[256,3584]{1,0:T(8,128)(2,1)S(1)}, bf16[256,3584]{1,0:T(8,128)(2,1)}, u32[]{:S(2)}) copy-start(bf16[256,3584]{1,0:T(8,128)(2,1)} %param.13) | copy-start | bytes 5505028
  131.6 42.2 %copy-start.6 = (f32[896]{0:T(1024)S(1)}, f32[896]{0:T(1024)}, u32[]{:S(2)}) copy-start(f32[896]{0:T(1024)} %param.23) | copy-start | bytes 10756
Sparse Core Ops, SparseCore 0:
  135.7 30.7 reduce-scatter.3
where the time goes:
time: 212 us; the launch traced here: 211 us
  blocking collectives  100 us (47%)
  waiting for transfers between devices  30.9 us (15%)
  matrix products  29.3 us (14%)
  other arithmetic  18.1 us (9%)
  local copies, waits for them, and re-layouts  16.8 us (8%)
  between operations  15.6 us (7%)
    all_gather x1, blocking collectives, body(): lax.all_gather(keys, 'seq', axis=0, tiled=True)  33.5 us
    all_gather x1, blocking collectives, body(): lax.all_gather(values, 'seq', axis=0, tiled=True)  33.4 us
    unnamed x2, waiting for transfers between devices  30.9 us
    psum x1, blocking collectives, body(): pooled_sum = lax.psum(local_sum, 'seq')  21.5 us
    reduce_sum x1, other arithmetic, absorb(): total = jnp.sum(weights, axis=1)  8.15 us
    dot_general x1, matrix products, key_scores(): lax.dot_general(queries, key_block, (((1,), (1,)), ((), ())), preferred_e...  7.28 us
    dot_general x1, matrix products, absorb(): jnp.dot(weights.astype(jnp.bfloat16), v_piece, preferred_element_type=jnp...  6.61 us
    dot_general x1, matrix products, body(): jnp.dot(normed, q_weight, preferred_element_type=jnp.float32) + q_bias  6.46 us
  transfers between devices with their start and end apart: 1, of which 1 were waited for; matrix products, arithmetic and copies ran while one was open for 0% of the time, Pallas kernels for 0%

commit v1 on v0

--- a/solution.py
+++ b/solution.py
@@ -113,7 +113,11 @@
     final = hidden_full * lax.rsqrt(squares[:, None] / D + epsilon) * final_gain
     row_live = positions < limit
     local_sum = jnp.sum(jnp.where(row_live[:, None], final, 0.0), axis=0)
-    pooled_sum = lax.psum(local_sum, "seq")
+    pooled_sum = local_sum
+    for hop in (1, 2, 4):
+        pooled_sum = pooled_sum + lax.ppermute(
+            pooled_sum, "seq", [(dev, dev ^ hop) for dev in range(8)]
+        )
     mean = pooled_sum / limit.astype(jnp.float32)
     power = lax.psum(jnp.sum(mean * mean), "head")
     embedding = mean * lax.rsqrt(power / D + epsilon)

time: 212 us -> 202 us (0.953)
  blocking collectives: 100 us -> 78.9 us
  starting transfers between devices: 0.04 us -> 5.96 us
  waiting for transfers between devices: 30.9 us -> 36.7 us
    psum x1 -> x0, blocking collectives: 21.5 us -> none  [body(): pooled_sum = lax.psum(local_sum, 'seq')]
    ppermute x0 -> x3, starting transfers between devices: none -> 5.93 us  [body(): lax.ppermute(pooled_sum, 'seq', [(dev, dev ^ hop) for dev in range(8)])]
    ppermute x0 -> x3, waiting for transfers between devices: none -> 5.79 us  [body(): lax.ppermute(pooled_sum, 'seq', [(dev, dev ^ hop) for dev in range(8)])]
  transfers between devices with their start and end apart: 1 -> 4, of which waited for: 1 -> 4; matrix products, arithmetic and copies ran while one was open for 0% -> 0% of each run, Pallas kernels for 0% -> 0%
where the time goes in v1:
time: 202 us
  blocking collectives  78.9 us (39%)
  waiting for transfers between devices  36.7 us (18%)
  matrix products  29.3 us (15%)
  other arithmetic  18.1 us (9%)
  local copies, waits for them, and re-layouts  16.8 us (8%)
  between operations  15.6 us (8%)
  starting transfers between devices  5.96 us (3%)
    all_gather x1, blocking collectives, body(): lax.all_gather(keys, 'seq', axis=0, tiled=True)  33.5 us
    all_gather x1, blocking collectives, body(): lax.all_gather(values, 'seq', axis=0, tiled=True)  33.4 us
    unnamed x2, waiting for transfers between devices  30.9 us
    reduce_sum x1, other arithmetic, absorb(): total = jnp.sum(weights, axis=1)  8.15 us
    dot_general x1, matrix products, key_scores(): lax.dot_general(queries, key_block, (((1,), (1,)), ((), ())), preferred_e...  7.28 us
    dot_general x1, matrix products, absorb(): jnp.dot(weights.astype(jnp.bfloat16), v_piece, preferred_element_type=jnp...  6.61 us
    dot_general x1, matrix products, body(): jnp.dot(normed, q_weight, preferred_element_type=jnp.float32) + q_bias  6.46 us
    psum x1, blocking collectives, body(): power = lax.psum(jnp.sum(mean * mean), 'head')  6.27 us
  transfers between devices with their start and end apart: 4, of which 4 were waited for; matrix products, arithmetic and copies ran while one was open for 0% of the time, Pallas kernels for 0%

profile of v1, /device:TPU:0, one launch (start us, length us, event | category | flops | bytes accessed | tf_op | source)
XLA Modules:
  0.0 201.5 jit_solution(4795228894830560779)
XLA Ops:
  7.2 2.0 fusion.7
  9.3 6.5 %convolution_add_fusion = f32[256,896]{1,0:T(8,128)} fusion(bf16[3584,896]{1,0:T(8,128)(2,1)} %param.16, f32[896]{0:T(1024)} %param.17, bf16[256,3584]{1,0:T(8,128)(2,1)} %param.13, f32[3584]{0:T(1024)} %param.15, f32[256]{0:T(256)S(1)} %add_rsqrt_fusion.1), kind=kOutput, calls=%fused_computation.16 | convolution fusion | flops 1648066560 | bytes 9193984 | tf_op jit(solution)/shard_map/dot_general | solution.py:57
  15.7 2.6 %copy.23 = f32[256,896]{0,1:T(8,128)} copy(f32[256,896]{1,0:T(8,128)} %convolution_add_fusion) | data formatting | bytes 1835008 | tf_op jit(solution)/shard_map/add | solution.py:57
  18.3 2.2 %reshape.119 = f32[1792,128]{1,0:T(8,128)} reshape(f32[256,896]{1,0:T(8,128)} %convolution_add_fusion) | data formatting | bytes 1835008 | tf_op jit(solution)/shard_map/reshape | solution.py:58
  23.5 33.5 %all_gather.6 = bf16[2048,128]{0,1:T(8,128)(2,1)S(1)} all-gather(bf16[256,128]{0,1:T(8,128)(2,1)} %get-tuple-element.38), channel_id=1, replica_groups=mesh['seq'=8,'head'=4] {'seq'}, dimensions={0}, use_global_device_ids=true | all-gather | bytes 589824 | tf_op jit(solution)/shard_map/all_gather | solution.py:89
  57.0 1.9 fusion.10
  58.9 33.4 %all_gather.7 = bf16[2048,128]{1,0:T(8,128)(2,1)} all-gather(bf16[256,128]{1,0:T(8,128)(2,1)S(1)} %fusion.10), channel_id=1, replica_groups=mesh['seq'=8,'head'=4] {'seq'}, dimensions={0}, use_global_device_ids=true | all-gather | bytes 589824 | tf_op jit(solution)/shard_map/all_gather | solution.py:90
  96.8 1.4 copy.25
  99.3 2.4 %fusion.13 = bf16[1792,128]{1,0:T(8,128)(2,1)S(1)} fusion(f32[1792,128]{1,0:T(8,128)} %mul.134, f32[1792,64]{1,0:T(8,128)} %concatenate.29, f32[1792,64]{1,0:T(8,128)} %concatenate.28, f32[1792,128]{1,0:T(8,128)S(1)} %copy-done.3, f32[1792,128]{1,0:T(8,128)} %mul.131), kind=kLoop, calls=%fused_computation.23 | loop fusion | flops 1376256 | bytes 4128768 | tf_op jit(solution)/shard_map/convert_element_type | solution.py:59
  101.7 22.9 %conditional.1 = (f32[1792]{0:T(1024)S(1)}, f32[1792,128]{1,0:T(8,128)S(1)}) conditional(s32[]{:T(128)} %convert_element_type.49, () %tuple.16, (s32[]{:T(128)}, bf16[1792,128]{1,0:T(8,128)(2,1)S(1)}, bf16[2048,128]{0,1:T(8,128)(2,1)S(1)}, bf16[2048,128]{1,0:T(8,128)(2,1)S(1)}) %tuple.32), branch_computations={%region_1.0_spmd, %region_2.5_spmd} | conditional | flops 1915748608 | bytes 46516244 | solution.py:99
  102.6 7.3 %select_reduce_fusion = (f32[1792]{0:T(1024)S(1)}, f32[1792,2048]{1,0:T(8,128)}) fusion(pred[2048]{0:T(1024)(128)(4,1)S(1)} %iota_compare_fusion, bf16[1792,128]{1,0:T(8,128)(2,1)S(1)} %get-tuple-element.9, bf16[2048,128]{0,1:T(8,128)(2,1)S(1)} %get-tuple-element.28), kind=kOutput, calls=%fused_computation.1 | convolution fusion | flops 946862336 | bytes 15672320 | tf_op jit(solution)/shard_map/cond/branch_1_fun/dot_general | solution.py:32
  109.9 8.2 %fusion.1 = f32[1792]{0:T(1024)S(1)} fusion(f32[1792,2048]{1,0:T(8,128)} %get-tuple-element.31, f32[1792]{0:T(1024)S(1)} %broadcast_maximum_fusion, pred[2048]{0:T(1024)(128)(4,1)S(1)} %iota_compare_fusion), kind=kLoop, calls=%fused_computation.3 | loop fusion | flops 14678272 | bytes 14696448 | tf_op jit(solution)/shard_map/cond/branch_1_fun/reduce_sum | solution.py:79
  118.0 6.6 %fusion.2 = f32[1792,128]{1,0:T(8,128)S(1)} fusion(bf16[2048,128]{1,0:T(8,128)(2,1)S(1)} %get-tuple-element.11, f32[1792,2048]{1,0:T(8,128)} %get-tuple-element.31, f32[1792]{0:T(1024)S(1)} %broadcast_maximum_fusion, pred[2048]{0:T(1024)(128)(4,1)S(1)} %iota_compare_fusion), kind=kOutput, calls=%fused_computation.4 | convolution fusion | flops 954204160 | bytes 16131072 | tf_op jit(solution)/shard_map/cond/branch_1_fun/dot_general | solution.py:80
  125.4 6.1 %convolution_convert_fusion = bf16[256,3584]{1,0:T(8,128)(2,1)} fusion(bf16[256,896]{1,0:T(8,128)(2,1)S(1)} %reshape.122, bf16[896,3584]{1,0:T(8,128)(2,1)} %param.22), kind=kOutput, calls=%fused_computation.10 | convolution fusion | flops 1645084672 | bytes 8716288 | tf_op jit(solution)/shard_map/dot_general | solution.py:103
  131.6 4.0 %copy.29 = bf16[256,3584]{0,1:T(8,128)(2,1)} copy(bf16[256,3584]{1,0:T(8,128)(2,1)} %convolution_convert_fusion) | data formatting | bytes 3670016
  135.6 30.9 %reduce-scatter.4.cloned.1.call-done = bf16[896,256]{1,0:T(8,128)(2,1)} async-done(((bf16[3584,256]{1,0:T(8,128)(2,1)}), bf16[896,256]{1,0:T(8,128)(2,1)}) %reduce-scatter.4.cloned.1.call-update) | async-done | bytes 458768
  168.0 5.8 %psum.14 = f32[256]{0:T(256)S(1)} all-reduce(f32[256]{0:T(256)S(1)} %multiply_reduce_fusion), channel_id=1, replica_groups=mesh['seq'=8,'head'=4] {'head'}, use_global_device_ids=true, to_apply=%region_7.8 | all-reduce | flops 256 | bytes 2048 | tf_op jit(solution)/shard_map/psum | solution.py:112
  174.8 1.6 collective-permute-start
  176.4 2.0 collective-permute-done
  178.4 1.7 collective-permute-start.1
  180.1 1.9 collective-permute-done.1
  182.0 2.6 %collective-permute-start.2 = (f32[896]{0:T(1024)S(1)}, f32[896]{0:T(1024)S(1)}, u32[]{:S(2)}, u32[]{:S(2)}) collective-permute-start(f32[896]{0:T(1024)S(1)} %add.96), channel_id=1, source_target_pairs={{0,16},{4,20},{8,24},{12,28},{16,0},{20,4},{24,8},{28,12},{1,17},{... | collective-permute-start | bytes 10760 | tf_op jit(solution)/shard_map/ppermute | solution.py:118
  184.6 1.9 collective-permute-done.2
  187.1 6.3 %psum.15 = f32[]{:T(128)} all-reduce(f32[]{:T(128)} %multiply_reduce_fusion.1), channel_id=1, replica_groups=mesh['seq'=8,'head'=4] {'head'}, use_global_device_ids=true, to_apply=%region_10.11 | all-reduce | flops 1 | bytes 8 | tf_op jit(solution)/shard_map/psum | solution.py:122
  (52 shorter events, 13.1 us)
Async XLA Ops:
  7.2 14.0 %copy-start = (bf16[3584,128]{1,0:T(8,128)(2,1)S(1)}, bf16[3584,128]{1,0:T(8,128)(2,1)}, u32[]{:S(2)}) copy-start(bf16[3584,128]{1,0:T(8,128)(2,1)} %param.18) | copy-start | bytes 2752516
  7.2 159.3 %reduce-scatter.4.cloned.1.call-start = ((), (), s32[]{:S(2)}) async-start(), calls=%async_computation.1 | async-start | bytes 2293760
  15.7 5.4 %copy-start.1 = (bf16[256,3584]{1,0:T(8,128)(2,1)S(1)}, bf16[256,3584]{1,0:T(8,128)(2,1)}, u32[]{:S(2)}) copy-start(bf16[256,3584]{1,0:T(8,128)(2,1)} %param.13) | copy-start | bytes 5505028
  15.7 5.5 %copy-start.7 = (f32[3584]{0:T(1024)S(1)}, f32[3584]{0:T(1024)}, u32[]{:S(2)}) copy-start(f32[3584]{0:T(1024)} %param.15) | copy-start | bytes 43012
  15.7 5.5 %copy-start.8 = (f32[128]{0:T(128)S(1)}, f32[128]{0:T(128)}, u32[]{:S(2)}) copy-start(f32[128]{0:T(128)} %param.19) | copy-start | bytes 1540
  18.3 38.7 %copy-start.9 = (f32[128]{0:T(128)S(1)}, f32[128]{0:T(128)}, u32[]{:S(2)}) copy-start(f32[128]{0:T(128)} %param.21) | copy-start | bytes 1540
  23.5 68.8 %copy-start.4 = (f32[256,896]{0,1:T(8,128)S(1)}, f32[256,896]{0,1:T(8,128)}, u32[]{:S(2)}) copy-start(f32[256,896]{0,1:T(8,128)} %copy.23) | copy-start | bytes 2752516
  95.7 3.6 %copy-start.3 = (f32[1792,128]{1,0:T(8,128)S(1)}, f32[1792,128]{1,0:T(8,128)}, u32[]{:S(2)}) copy-start(f32[1792,128]{1,0:T(8,128)} %reshape.119) | copy-start | bytes 2752516
  99.3 2.4 %copy-start.5 = (bf16[2048,128]{1,0:T(8,128)(2,1)S(1)}, bf16[2048,128]{1,0:T(8,128)(2,1)}, u32[]{:S(2)}) copy-start(bf16[2048,128]{1,0:T(8,128)(2,1)} %all_gather.7) | copy-start | bytes 1572868
  131.6 36.2 %copy-start.2 = (bf16[256,3584]{1,0:T(8,128)(2,1)S(1)}, bf16[256,3584]{1,0:T(8,128)(2,1)}, u32[]{:S(2)}) copy-start(bf16[256,3584]{1,0:T(8,128)(2,1)} %param.13) | copy-start | bytes 5505028
  131.6 42.2 %copy-start.6 = (f32[896]{0:T(1024)S(1)}, f32[896]{0:T(1024)}, u32[]{:S(2)}) copy-start(f32[896]{0:T(1024)} %param.23) | copy-start | bytes 10756
  174.8 3.6 %collective-permute-start = (f32[896]{0:T(1024)S(1)}, f32[896]{0:T(1024)S(1)}, u32[]{:S(2)}, u32[]{:S(2)}) collective-permute-start(f32[896]{0:T(1024)S(1)} %get-tuple-element.32), channel_id=1, source_target_pairs={{0,4},{4,0},{8,12},{12,8},{16,20},{20,16},{24,28},{28,24},{1,5},{5... | collective-permute-start | bytes 10760 | tf_op jit(solution)/shard_map/ppermute | solution.py:118
  178.4 3.6 %collective-permute-start.1 = (f32[896]{0:T(1024)S(1)}, f32[896]{0:T(1024)S(1)}, u32[]{:S(2)}, u32[]{:S(2)}) collective-permute-start(f32[896]{0:T(1024)S(1)} %add.95), channel_id=1, source_target_pairs={{0,8},{4,12},{8,0},{12,4},{16,24},{20,28},{24,16},{28,20},{1,9},{5... | collective-permute-start | bytes 10760 | tf_op jit(solution)/shard_map/ppermute | solution.py:118
  182.0 4.5 %collective-permute-start.2 = (f32[896]{0:T(1024)S(1)}, f32[896]{0:T(1024)S(1)}, u32[]{:S(2)}, u32[]{:S(2)}) collective-permute-start(f32[896]{0:T(1024)S(1)} %add.96), channel_id=1, source_target_pairs={{0,16},{4,20},{8,24},{12,28},{16,0},{20,4},{24,8},{28,12},{1,17},{... | collective-permute-start | bytes 10760 | tf_op jit(solution)/shard_map/ppermute | solution.py:118
Sparse Core Ops, SparseCore 0:
  135.7 30.7 reduce-scatter.3
